TPU v7x, 256 devices: a whole 4x4x8 slice. The times are simulated.
256 devices in a mesh: occ: 32 (over x, z_lo, core), aux: 8 (over y, z_hi).
Axes of the slice: x: 4, y: 4, z: 8 (z_hi: 2, z_lo: 4; z = z_hi * 4 + z_lo), core: 2. Of those that a mesh axis runs over, the one named last changes fastest.
Arguments:
- b_factors: bfloat16 [32, 256, 12288], P('occ', None, 'aux'), may hold values from -0.056884766 to 0.056884766
- occ_energies: float32 [32], P('occ'), may hold values from -1.2 to -0.3
- vir_energies: float32 [256], replicated, may hold values from 0.1 to 4
- pair_list: int32 [32, 48, 3], P('occ'), may hold values from -1 to 31, as said below
- pair_count: int32 [32], P('occ'), may hold values from 1 to 48, as said below
Outputs:
- pair_energy: float32 [32, 48], P('occ', 'aux')
- total_energy: float32 [], replicated
Inputs may be any that keep to these rules, and one draw needn't show every extreme that they name: `pair_list`: row i lists pair_count[i] distinct items (j, a-block, b-block) with j in 0 to 31 and blocks in 0 to 1, ordered by j, then a-block, then b-block; its other slots hold -1 in all three fields. `pair_count`: some occupied orbital lists exactly 48 items.
All inputs are finite; a program needn't handle non-finite values.
Results may differ from a plain program's by a relative error of at most 0.0003.
Values may be sent and summed in bfloat16 or wider, within the bound.
A program may use at most 128 MiB of HBM per device.

v0:
```python
import jax
import jax.numpy as jnp
from jax import lax
from jax.sharding import Mesh
from jax.sharding import PartitionSpec as P

VB = 128
OCC = ("occ_0", "occ_1", "occ_2")
AUX = ("aux_0", "aux_1")
OCC_AUX = ("occ_0", "occ_1", "occ_2", "aux_0", "aux_1")


def joined_along(pieces, dim):
    pieces = jnp.moveaxis(pieces, 0, dim)
    lengths = pieces.shape
    return pieces.reshape(*lengths[:dim], lengths[dim] * lengths[dim + 1], *lengths[dim + 2 :])


def sent_to_all(array, axis):
    count = lax.axis_size(axis)
    return lax.all_to_all(
        jnp.broadcast_to(array[None], (count, *array.shape)), axis, 0, 0, tiled=True
    )


def gathered_copies(array, axis, dim):
    return joined_along(sent_to_all(array, axis), dim)


def summed_rows(array, axes, dim):
    for axis in axes:
        array = lax.psum_scatter(array, axis, scatter_dimension=dim, tiled=True)
    return array


def by_axis(array, axes):
    for axis in axes:
        array = lax.psum(array, axis)
    return array


def local(b_factors, occ_energies, vir_energies, pair_list, pair_count):
    home_panel = b_factors[0]
    item_table = pair_list[0]
    slot_count = pair_count[0]
    slot_total = item_table.shape[0]
    virt_width = home_panel.shape[0]
    block_count = virt_width // VB
    live_slots = jnp.arange(slot_total, dtype=jnp.int32) < slot_count
    all_occ = gathered_copies(occ_energies, OCC, 0)
    cycle_width = lax.axis_size(OCC)
    shard_rows = b_factors.shape[0]
    orbital_total = cycle_width * shard_rows
    contract = (((1,), (2,)), ((), ()))
    block = lax.dot_general(
        home_panel,
        lax.all_gather(b_factors, OCC, axis=0, tiled=True),
        contract,
        preferred_element_type=jnp.float32,
    )
    block = jnp.transpose(block, (1, 0, 2))
    tiles = block.reshape(orbital_total, block_count, VB, block_count, VB)
    tiles = jnp.transpose(tiles, (0, 1, 3, 2, 4)).reshape(
        orbital_total * block_count * block_count, VB, VB
    )
    partner_ids = jnp.maximum(item_table[:, 0], 0)
    left_ids = jnp.maximum(item_table[:, 1], 0)
    right_ids = jnp.maximum(item_table[:, 2], 0)
    direct_code = (partner_ids * block_count + left_ids) * block_count + right_ids
    swapped_code = (partner_ids * block_count + right_ids) * block_count + left_ids
    direct_tiles = jnp.take(tiles, direct_code, axis=0)
    swapped_tiles = jnp.take(tiles, swapped_code, axis=0)
    tile_stack = jnp.stack([direct_tiles, swapped_tiles], axis=1)
    reduced = summed_rows(tile_stack, AUX, 0)
    aux_width = lax.axis_size(AUX)
    per_device = slot_total // aux_width
    share_start = lax.axis_index(AUX) * per_device
    my_items = lax.dynamic_slice_in_dim(item_table, share_start, per_device, 0)
    my_live = lax.dynamic_slice_in_dim(live_slots, share_start, per_device, 0)
    block_ids = jnp.arange(block_count, dtype=jnp.int32)
    virtual_blocks = vir_energies.reshape(block_count, VB)
    picks_left = (my_items[:, 1][:, None] == block_ids[None, :]).astype(jnp.float32)
    picks_right = (my_items[:, 2][:, None] == block_ids[None, :]).astype(jnp.float32)
    left_energy = jnp.dot(picks_left, virtual_blocks, precision=lax.Precision.HIGHEST)
    right_energy = jnp.dot(picks_right, virtual_blocks, precision=lax.Precision.HIGHEST)
    orbital_ids = jnp.arange(all_occ.shape[0], dtype=jnp.int32)
    partner_energy = jnp.sum(
        jnp.where(my_items[:, 0][:, None] == orbital_ids[None, :], all_occ[None, :], 0.0), axis=1
    )
    denominator = (
        left_energy[:, :, None]
        + right_energy[:, None, :]
        - occ_energies[0]
        - partner_energy[:, None, None]
    )
    direct = reduced[:, 0]
    swapped_back = jnp.transpose(reduced[:, 1], (0, 2, 1))
    energy = -jnp.sum(direct * (2.0 * direct - swapped_back) / denominator, axis=(1, 2))
    energy = jnp.where(my_live, energy, jnp.zeros_like(energy))
    total_energy = by_axis(jnp.sum(energy), OCC_AUX)
    return (energy[None, :], total_energy)


def solution(mesh):
    finer = Mesh(mesh.devices.reshape(4, 4, 2, 4, 2), ("occ_0", "occ_1", "occ_2", "aux_0", "aux_1"))
    placed = (P(OCC, None, AUX), P(OCC), P(), P(OCC, None, None), P(OCC))
    return jax.shard_map(
        local, mesh=finer, in_specs=placed, out_specs=(P(OCC, AUX), P()), check_vma=False
    )
```

profile of v0, /device:TPU:32, one launch (start us, length us, event | category | flops | bytes accessed | tf_op | source)
XLA Modules:
  0.0 493.4 jit_solution(6576529788671518339)
XLA Ops:
  7.2 0.7 all-gather.2.cloned.1.call-update
  8.0 0.7 copy.26
  8.7 145.7 %all-gather.2.cloned.1.call-done = bf16[32,256,1536]{2,1,0:T(8,128)(2,1)} async-done(((bf16[1,256,1536]{2,1,0:T(8,128)(2,1)}), bf16[32,256,1536]{2,1,0:T(8,128)(2,1)}) %all-gather.2.cloned.1.call-update) | async-done | bytes 25165840 | tf_op jit(solution)/shard_map/all_gather | solution.py:57
  154.4 13.8 %convolution_bitcast_fusion = f32[32,256,256]{2,1,0:T(8,128)} fusion(bf16[32,256,1536]{2,1,0:T(8,128)(2,1)} %all-gather.2.cloned.1.call-done, bf16[1,256,1536]{2,1,0:T(8,128)(2,1)} %param.7), kind=kOutput, calls=%fused_computation.3 | convolution fusion | flops 6442450944 | bytes 34340864 | tf_op jit(solution)/shard_map/dot_general | solution.py:55
  168.2 10.8 %reshape.37 = f32[32,2,128,2,128]{4,3,2,1,0:T(2,128)} reshape(f32[32,256,256]{2,1,0:T(8,128)} %convolution_bitcast_fusion) | data formatting | bytes 16777216 | tf_op jit(solution)/shard_map/reshape | solution.py:62
  178.9 7.8 %copy.14 = f32[32,2,128,2,128]{4,2,3,1,0:T(8,128)} copy(f32[32,2,128,2,128]{4,3,2,1,0:T(2,128)} %reshape.37) | data formatting | bytes 16777216 | tf_op jit(solution)/shard_map/reshape | solution.py:62
  186.7 4.1 gather_fusion.1
  190.8 5.8 %gather_fusion = f32[48,128,128]{2,1,0:T(8,128)} fusion(f32[128,128,128]{2,1,0:T(8,128)} %bitcast.102, s32[1024]{0:T(1024)S(1)} %pad_clamp_fusion.1), kind=kCustom, calls=%fused_computation.clone | custom fusion | bytes 6291648 | tf_op jit(solution)/shard_map/jit(_take)/gather | solution.py:71
  196.6 2.4 select_bitcast_fusion
  199.0 3.4 pad_maximum_fusion
  204.3 131.1 %all-reduce.5.cloned.1.call-done = f32[48,2,128,128]{3,2,0,1:T(8,128)} async-done(((f32[48,2,128,128]{3,2,0,1:T(8,128)}), f32[48,2,128,128]{3,2,0,1:T(8,128)}) %all-reduce.5.cloned.1.call-update) | async-done | bytes 6291472
  335.4 2.7 constant_dynamic-slice_fusion.1
  338.7 0.6 broadcast_in_dim.38
  339.4 7.9 %all-to-all-start = ((f32[32,1,1]{2,1,0:T(1,128)}), f32[32,1,1]{2,1,0:T(1,128)S(1)}, u32[]{:S(2)}, u32[]{:S(2)}) async-start(f32[32,1,1]{2,1,0:T(1,128)} %broadcast_in_dim.38), calls=%async_computation | async-start | bytes 32768 | tf_op jit(solution)/shard_map/all_to_all | solution.py:21
  349.6 4.1 all-to-all-done
  354.2 83.9 %all-reduce.7.cloned.1.call-done = f32[12,2,128,128]{3,2,0,1:T(8,128)} async-done(((f32[12,2,128,128]{3,2,0,1:T(8,128)}), f32[12,2,128,128]{3,2,0,1:T(8,128)}) %all-reduce.7.cloned.1.call-update) | async-done | bytes 1572880
  438.1 1.0 constant_dynamic-slice_fusion
  439.3 1.3 fusion.4
  440.6 1.2 fusion.14
  441.7 11.0 %psum.35 = f32[]{:T(128)} all-reduce(f32[]{:T(128)} %get-tuple-element.3), channel_id=1, replica_groups=mesh['occ_0'=4,'occ_1'=4,'occ_2'=2,'aux_0'=4,'aux_1'=2] {'occ_0'}, use_global_device_ids=true, to_apply=%region_5.7 | all-reduce | flops 1 | bytes 8 | tf_op jit(solution)/shard_map/psum | solution.py:38
  452.8 10.4 %psum.36 = f32[]{:T(128)} all-reduce(f32[]{:T(128)} %psum.35), channel_id=1, replica_groups=mesh['occ_0'=4,'occ_1'=4,'occ_2'=2,'aux_0'=4,'aux_1'=2] {'occ_1'}, use_global_device_ids=true, to_apply=%region_6.8 | all-reduce | flops 1 | bytes 8 | tf_op jit(solution)/shard_map/psum | solution.py:38
  463.2 3.1 psum.37
  466.3 11.1 %psum.38 = f32[]{:T(128)} all-reduce(f32[]{:T(128)} %psum.37), channel_id=1, replica_groups=mesh['occ_0'=4,'occ_1'=4,'occ_2'=2,'aux_0'=4,'aux_1'=2] {'aux_0'}, use_global_device_ids=true, to_apply=%region_8.10 | all-reduce | flops 1 | bytes 8 | tf_op jit(solution)/shard_map/psum | solution.py:38
  477.4 9.4 %psum.39 = f32[]{:T(128)} all-reduce(f32[]{:T(128)} %psum.38), channel_id=1, replica_groups=mesh['occ_0'=4,'occ_1'=4,'occ_2'=2,'aux_0'=4,'aux_1'=2] {'aux_1'}, use_global_device_ids=true, to_apply=%region_9.11 | all-reduce | flops 1 | bytes 8 | tf_op jit(solution)/shard_map/psum | solution.py:38
  (27 shorter events, 3.1 us)
Async XLA Ops:
  7.2 341.4 %copy-start = (f32[256]{0:T(256)S(1)}, f32[256]{0:T(256)}, u32[]{:S(2)}) copy-start(f32[256]{0:T(256)} %param.9) | copy-start | bytes 3076
  7.2 147.2 %all-gather.2.cloned.1.call-start = ((), (), s32[]{:S(2)}) async-start(), calls=%async_computation.1 | async-start | bytes 25952256 | tf_op jit(solution)/shard_map/all_gather | solution.py:57
  7.9 327.5 %all-reduce.5.cloned.1.call-start = ((), (), s32[]{:S(2)}) async-start(), calls=%async_computation.2 | async-start | bytes 12582912
  202.4 0.7 copy-start.3
  202.4 144.8 %copy-start.2 = (u32[256]{0:T(256)S(1)}, u32[256]{0:T(256)}, u32[]{:S(2)}) copy-start(u32[256]{0:T(256)} %constant.44) | copy-start | bytes 3076
  202.4 145.4 %copy-start.1 = (s32[1,48,3]{1,0,2:T(1,128)S(1)}, s32[1,48,3]{1,0,2:T(1,128)}, u32[]{:S(2)}) copy-start(s32[1,48,3]{1,0,2:T(1,128)} %param.10) | copy-start | bytes 1732
  202.4 235.6 %all-reduce.7.cloned.1.call-start = ((), (), s32[]{:S(2)}) async-start(), calls=%async_computation.3 | async-start | bytes 3145728
  339.4 14.3 %all-to-all-start = ((f32[32,1,1]{2,1,0:T(1,128)}), f32[32,1,1]{2,1,0:T(1,128)S(1)}, u32[]{:S(2)}, u32[]{:S(2)}) async-start(f32[32,1,1]{2,1,0:T(1,128)} %broadcast_in_dim.38), calls=%async_computation | async-start | bytes 32768 | tf_op jit(solution)/shard_map/all_to_all | solution.py:21
Sparse Core Ops, SparseCore 0:
  9.8 144.4 all-gather.1
  202.5 132.7 all-reduce.4
  338.2 99.8 all-reduce.6
where the time goes:
time: 494 us; the launch traced here: 493 us
  waiting for transfers between devices  365 us (74%)
  blocking collectives  45.1 us (9%)
  local copies, waits for them, and re-layouts  35.5 us (7%)
  between operations  16.5 us (3%)
  matrix products  14.1 us (3%)
  other arithmetic  8.77 us (2%)
  starting transfers between devices  7.97 us (2%)
    unnamed x5, waiting for transfers between devices  216 us
    all_gather x1, waiting for transfers between devices, local(): lax.all_gather(b_factors, OCC, axis=0, tiled=True)  146 us
    psum x5, blocking collectives, by_axis(): array = lax.psum(array, axis)  45.1 us
    reshape x2, local copies, waits for them, and re-layouts, local(): tiles = block.reshape(orbital_total, block_count, VB, block_count, VB)  18.5 us
    dot_general x1, matrix products, local(): lax.dot_general(home_panel, lax.all_gather(b_factors, OCC, axis=0, tiled=...  13.8 us
  transfers between devices with their start and end apart: 4, of which 4 were waited for; matrix products, arithmetic and copies ran while one was open for 1% of the time, Pallas kernels for 0%

commit v1 on v0

--- a/solution.py
+++ b/solution.py
@@ -8,6 +8,13 @@
 OCC = ("occ_0", "occ_1", "occ_2")
 AUX = ("aux_0", "aux_1")
 OCC_AUX = ("occ_0", "occ_1", "occ_2", "aux_0", "aux_1")
+
+
+def gather_over(shard, name, dim):
+    size = lax.axis_size(name)
+    parts = jnp.stack([shard for _ in range(size)])
+    parts = lax.all_to_all(parts, name, split_axis=0, concat_axis=0)
+    return jnp.concatenate(parts, axis=dim)
 
 
 def joined_along(pieces, dim):
@@ -53,10 +60,7 @@
     orbital_total = cycle_width * shard_rows
     contract = (((1,), (2,)), ((), ()))
     block = lax.dot_general(
-        home_panel,
-        lax.all_gather(b_factors, OCC, axis=0, tiled=True),
-        contract,
-        preferred_element_type=jnp.float32,
+        home_panel, gather_over(b_factors, OCC, 0), contract, preferred_element_type=jnp.float32
     )
     block = jnp.transpose(block, (1, 0, 2))
     tiles = block.reshape(orbital_total, block_count, VB, block_count, VB)

time: 494 us -> 908 us (1.84)
  waiting for transfers between devices: 365 us -> 761 us
    all_to_all x0 -> x1, waiting for transfers between devices: none -> 540 us  [gather_over(): parts = lax.all_to_all(parts, name, split_axis=0, concat_axis=0)]
    all_gather x1 -> x0, waiting for transfers between devices: 146 us -> none  [local(): lax.all_gather(b_factors, OCC, axis=0, tiled=True)]
    another operation x0 -> x1, local copies, waits for them, and re-layouts: none -> 9.54 us  [gather_over(): parts = jnp.stack([shard for _ in range(size)])]
    unnamed x5 -> x4, waiting for transfers between devices: 216 us -> 218 us
  transfers between devices with their start and end apart: 4 -> 4, of which waited for: 4 -> 4; matrix products, arithmetic and copies ran while one was open for 1% -> 0% of each run, Pallas kernels for 0% -> 0%
where the time goes in v1:
time: 908 us; the launch traced here: 907 us
  waiting for transfers between devices  761 us (84%)
  blocking collectives  45.1 us (5%)
  local copies, waits for them, and re-layouts  44.3 us (5%)
  between operations  16.8 us (2%)
  starting transfers between devices  16.7 us (2%)
  matrix products  13.9 us (2%)
    all_to_all x1, waiting for transfers between devices, gather_over(): parts = lax.all_to_all(parts, name, split_axis=0, concat_axis=0)  540 us
    unnamed x4, waiting for transfers between devices  218 us
    psum x5, blocking collectives, by_axis(): array = lax.psum(array, axis)  45.1 us
    reshape x2, local copies, waits for them, and re-layouts, local(): tiles = block.reshape(orbital_total, block_count, VB, block_count, VB)  18.5 us
  transfers between devices with their start and end apart: 4, of which 4 were waited for; matrix products, arithmetic and copies ran while one was open for 0% of the time, Pallas kernels for 0%

profile of v1, /device:TPU:32, one launch (start us, length us, event | category | flops | bytes accessed | tf_op | source)
XLA Modules:
  0.0 907.1 jit_solution(14793306959161622840)
XLA Ops:
  7.2 9.5 %stack.8 = bf16[32,1,256,1536]{3,2,1,0:T(8,128)(2,1)} broadcast(bf16[256,1536]{1,0:T(8,128)(2,1)} %bitcast.107), dimensions={2,3} | broadcast | bytes 25952256 | tf_op jit(solution)/shard_map/stack | solution.py:15
  16.7 8.8 all-to-all-start
  25.6 539.7 %all-to-all-done = bf16[32,1,256,1536]{3,2,1,0:T(8,128)(2,1)} async-done(((bf16[32,1,256,1536]{3,2,1,0:T(8,128)(2,1)}), bf16[32,1,256,1536]{3,2,1,0:T(8,128)(2,1)}, u32[]{:S(2)}, u32[]{:S(2)}) %all-to-all-start) | async-done | bytes 25165856 | tf_op jit(solution)/shard_map/all_to_all | solution.py:16
  565.4 13.6 %fusion.2 = f32[32,256,256]{2,1,0:T(8,128)} fusion(bf16[32,1,256,1536]{3,2,1,0:T(8,128)(2,1)} %all-to-all-done, bf16[1,256,1536]{2,1,0:T(8,128)(2,1)S(1)} %copy-done.1), kind=kOutput, calls=%fused_computation.5 | convolution fusion | flops 6442450944 | bytes 34340864 | tf_op jit(solution)/shard_map/dot_general | solution.py:62
  578.9 10.8 %reshape.44 = f32[32,2,128,2,128]{4,3,2,1,0:T(2,128)} reshape(f32[32,256,256]{2,1,0:T(8,128)} %fusion.2) | data formatting | bytes 16777216 | tf_op jit(solution)/shard_map/reshape | solution.py:66
  589.7 7.8 copy.14
  597.4 4.1 gather_fusion.1
  601.6 5.8 gather_fusion
  607.4 2.4 select_bitcast_fusion
  609.8 3.4 pad_maximum_fusion
  615.1 133.7 %all-reduce.5.cloned.1.call-done = f32[48,2,128,128]{3,2,0,1:T(8,128)} async-done(((f32[48,2,128,128]{3,2,0,1:T(8,128)}), f32[48,2,128,128]{3,2,0,1:T(8,128)}) %all-reduce.5.cloned.1.call-update) | async-done | bytes 6291472
  748.8 2.7 constant_dynamic-slice_fusion.1
  752.2 0.6 broadcast_in_dim.38
  752.8 7.9 all-to-all-start.1
  763.1 4.1 all-to-all-done.1
  767.6 83.9 %all-reduce.7.cloned.1.call-done = f32[12,2,128,128]{3,2,0,1:T(8,128)} async-done(((f32[12,2,128,128]{3,2,0,1:T(8,128)}), f32[12,2,128,128]{3,2,0,1:T(8,128)}) %all-reduce.7.cloned.1.call-update) | async-done | bytes 1572880
  851.5 1.0 constant_dynamic-slice_fusion
  852.7 1.3 fusion.9
  854.0 1.2 fusion.19
  855.2 11.0 %psum.35 = f32[]{:T(128)} all-reduce(f32[]{:T(128)} %get-tuple-element.3), channel_id=1, replica_groups=mesh['occ_0'=4,'occ_1'=4,'occ_2'=2,'aux_0'=4,'aux_1'=2] {'occ_0'}, use_global_device_ids=true, to_apply=%region_5.7 | all-reduce | flops 1 | bytes 8 | tf_op jit(solution)/shard_map/psum | solution.py:45
  866.2 10.4 %psum.36 = f32[]{:T(128)} all-reduce(f32[]{:T(128)} %psum.35), channel_id=1, replica_groups=mesh['occ_0'=4,'occ_1'=4,'occ_2'=2,'aux_0'=4,'aux_1'=2] {'occ_1'}, use_global_device_ids=true, to_apply=%region_6.8 | all-reduce | flops 1 | bytes 8 | tf_op jit(solution)/shard_map/psum | solution.py:45
  876.6 3.1 psum.37
  879.7 11.1 %psum.38 = f32[]{:T(128)} all-reduce(f32[]{:T(128)} %psum.37), channel_id=1, replica_groups=mesh['occ_0'=4,'occ_1'=4,'occ_2'=2,'aux_0'=4,'aux_1'=2] {'aux_0'}, use_global_device_ids=true, to_apply=%region_8.10 | all-reduce | flops 1 | bytes 8 | tf_op jit(solution)/shard_map/psum | solution.py:45
  890.8 9.4 %psum.39 = f32[]{:T(128)} all-reduce(f32[]{:T(128)} %psum.38), channel_id=1, replica_groups=mesh['occ_0'=4,'occ_1'=4,'occ_2'=2,'aux_0'=4,'aux_1'=2] {'aux_1'}, use_global_device_ids=true, to_apply=%region_9.11 | all-reduce | flops 1 | bytes 8 | tf_op jit(solution)/shard_map/psum | solution.py:45
  (29 shorter events, 3.0 us)
Async XLA Ops:
  7.2 754.8 %copy-start = (f32[256]{0:T(256)S(1)}, f32[256]{0:T(256)}, u32[]{:S(2)}) copy-start(f32[256]{0:T(256)} %param.9) | copy-start | bytes 3076
  16.7 8.9 copy-start.2
  16.7 548.6 %copy-start.1 = (bf16[1,256,1536]{2,1,0:T(8,128)(2,1)S(1)}, bf16[1,256,1536]{2,1,0:T(8,128)(2,1)}, u32[]{:S(2)}) copy-start(bf16[1,256,1536]{2,1,0:T(8,128)(2,1)} %param.7) | copy-start | bytes 2359300
  16.7 548.6 %all-to-all-start = ((bf16[32,1,256,1536]{3,2,1,0:T(8,128)(2,1)}), bf16[32,1,256,1536]{3,2,1,0:T(8,128)(2,1)}, u32[]{:S(2)}, u32[]{:S(2)}) async-start(bf16[32,1,256,1536]{3,2,1,0:T(8,128)(2,1)} %stack.8), calls=%async_computation | async-start | bytes 50331648 | tf_op jit(solution)/shard_map/all_to_all | solution.py:16
  25.5 723.3 %all-reduce.5.cloned.1.call-start = ((), (), s32[]{:S(2)}) async-start(), calls=%async_computation.2 | async-start | bytes 12582912
  613.1 0.7 copy-start.4
  613.2 147.5 %copy-start.3 = (u32[256]{0:T(256)S(1)}, u32[256]{0:T(256)}, u32[]{:S(2)}) copy-start(u32[256]{0:T(256)} %constant.44) | copy-start | bytes 3076
  613.2 238.3 %all-reduce.7.cloned.1.call-start = ((), (), s32[]{:S(2)}) async-start(), calls=%async_computation.3 | async-start | bytes 3145728
  752.8 14.3 %all-to-all-start.1 = ((f32[32,1,1]{2,1,0:T(1,128)}), f32[32,1,1]{2,1,0:T(1,128)S(1)}, u32[]{:S(2)}, u32[]{:S(2)}) async-start(f32[32,1,1]{2,1,0:T(1,128)} %broadcast_in_dim.38), calls=%async_computation.1 | async-start | bytes 32768 | tf_op jit(solution)/shard_map/all_to_all | solution.py:28
Sparse Core Ops, SparseCore 0:
  613.3 135.4 all-reduce.4
  751.6 99.8 all-reduce.6
